TPU v7x, 128 devices: a whole 4x4x4 slice. The times are simulated.
128 devices in a mesh: cp: 4 (over x), dp: 32 (over z, y, core).
Axes of the slice: x: 4, y: 4, z: 4, core: 2. Of those that a mesh axis runs over, the one named last changes fastest.
Arguments:
- tokens: bfloat16 [32, 1536, 7168], P('dp', 'cp')
- choices: int32 [32, 1536, 8], P('dp', 'cp')
- router_w: float32 [256, 7168], replicated
- expert_bias: float32 [256], replicated
Outputs:
- output 1: float32 [], replicated
- output 2: float32 [256, 7168], replicated
- output 3: bfloat16 [32, 1536, 7168], P('dp', 'cp')
- output 4: float32 [256], replicated
All inputs are finite; a program needn't handle non-finite values.
Results may differ from a plain program's by a relative error of at most 0.001.
Values sent between devices are 32-bit elements.
A program may use at most 1 GiB of HBM per device.

v0:
```python
import jax
import jax.numpy as jnp
from jax import lax
from jax.sharding import PartitionSpec as P

ALPHA = 0.1
GAMMA = 0.001
PRECISE = lax.Precision.HIGHEST


def solution(mesh):
    cp_size = mesh.shape["cp"]
    dp_size = mesh.shape["dp"]

    def local_step(tokens, choices, router_w, expert_bias):
        rows_all = tokens.shape[0] * dp_size
        seq_all = tokens.shape[1] * cp_size
        experts = router_w.shape[0]
        choice_num = choices.shape[2]
        expert_ids = jnp.arange(experts, dtype=jnp.int32)
        piece_counts = jnp.sum((choices[..., None] == expert_ids).astype(jnp.float32), axis=(1, 2))
        seq_counts = lax.psum(piece_counts, "cp")
        logits = jnp.einsum("bsd,nd->bsn", tokens, router_w, precision=PRECISE, preferred_element_type=jnp.float32)
        sig_probs = jax.nn.sigmoid(logits)
        prob_total = jnp.sum(sig_probs, axis=-1, keepdims=True)
        normed = sig_probs / prob_total
        prob_sums = lax.psum(jnp.sum(normed, axis=1), "cp")
        loss_scale = ALPHA * experts / (rows_all * choice_num * seq_all * seq_all)
        weight = seq_counts * loss_scale
        bal_loss = lax.psum(jnp.sum(weight * prob_sums), "dp")
        mixed_grad = jnp.sum(normed * weight[:, None, :], axis=-1, keepdims=True)
        grad_logits = (weight[:, None, :] - mixed_grad) * (sig_probs * (1.0 - sig_probs) / prob_total)
        grad_tokens = jnp.einsum("bsn,nd->bsd", grad_logits, router_w, precision=PRECISE, preferred_element_type=jnp.float32).astype(jnp.bfloat16)
        grad_part = jnp.einsum("bsn,bsd->nd", grad_logits, tokens, precision=PRECISE, preferred_element_type=jnp.float32)
        grad_router = lax.psum(grad_part, ("cp", "dp"))
        global_load = lax.psum(jnp.sum(seq_counts, axis=0), "dp")
        load_gap = rows_all * seq_all * choice_num - experts * global_load.astype(jnp.int32)
        new_bias = expert_bias + GAMMA * jnp.sign(load_gap).astype(jnp.float32)
        return bal_loss, grad_router, grad_tokens, new_bias

    tok_spec = P("dp", "cp", None)
    return jax.shard_map(local_step, mesh=mesh, in_specs=(tok_spec, tok_spec, P(), P()), out_specs=(P(), P(), tok_spec, P()), check_vma=False)
```

profile of v0, /device:TPU:1, one launch (start us, length us, event | category | flops | bytes accessed | tf_op | source)
XLA Modules:
  0.0 216.0 jit_solution(5432714754533539918)
XLA Ops:
  7.2 0.0 slice-start
  7.2 0.0 all-reduce.3.cloned.1.call-start
  7.2 0.9 copy.9
  8.2 0.6 convert_reduce_fusion
  8.7 9.3 %psum.35 = f32[1,256]{1,0:T(1,128)S(1)} all-reduce(f32[1,256]{1,0:T(1,128)S(1)} %bitcast.30), channel_id=1, replica_groups=mesh['cp'=4,'dp'=32] {'cp'}, use_global_device_ids=true, to_apply=%region_1.0 | all-reduce | flops 256 | bytes 2048 | tf_op jit(solution)/shard_map/psum | solution.py:22
  18.0 0.0 slice-start.1
  18.0 13.5 %fusion.16 = (f32[384]{0:T(512)S(1)}, f32[384,256]{0,1:T(8,128)S(1)}) fusion(f32[256,7168]{1,0:T(8,128)} %param.6, bf16[1,384,7168]{2,1,0:T(8,128)(2,1)} %param.4), kind=kOutput, calls=%fused_computation.17 | convolution fusion | flops 8456109568 | bytes 13239808 | tf_op jit(solution)/shard_map/bsd,nd->bsn/dot_general | solution.py:23
  31.6 0.2 multiply_reduce_fusion
  31.8 0.0 slice-done
  31.8 0.0 slice-done.1
  31.8 0.0 copy-start
  31.8 8.1 %fusion.1 = f32[256,7168]{1,0:T(8,128)} fusion(bf16[1,384,7168]{2,1,0:T(8,128)(2,1)S(1)} %bitcast.23, f32[384]{0:T(512)S(1)} %get-tuple-element.4, f32[256]{0:T(256)S(1)} %bitcast.25, f32[384]{0:T(512)S(1)} %get-tuple-element.8, f32[384,256]{0,1:T(8,128)S(1)} %get-tuple-element.9), kind=kOutput, calls=%fused_computation.2 | convolution fusion | flops 8456306688 | bytes 13242368 | tf_op jit(solution)/shard_map/bsn,bsd->nd/dot_general | solution.py:34
  39.9 0.0 all-reduce.3.cloned.1.call-update
  39.9 6.0 %psum.36 = f32[1,256]{1,0:T(1,128)S(1)} all-reduce(f32[1,256]{1,0:T(1,128)S(1)} %bitcast.29), channel_id=1, replica_groups=mesh['cp'=4,'dp'=32] {'cp'}, use_global_device_ids=true, to_apply=%region_4.0 | all-reduce | flops 256 | bytes 2048 | tf_op jit(solution)/shard_map/psum | solution.py:27
  45.9 0.6 multiply_reduce_fusion.1
  46.5 69.0 %all-reduce = (f32[]{:T(128)}, f32[256]{0:T(256)S(1)}) all-reduce(f32[]{:T(128)} %multiply_reduce_fusion.1, f32[256]{0:T(256)S(1)} %bitcast.28), channel_id=1, replica_groups=mesh['cp'=4,'dp'=32] {'dp'}, use_global_device_ids=true, to_apply=%region_6.0 | all-reduce | flops 257 | bytes 2056 | tf_op jit(solution)/shard_map/psum | solution.py:30
  115.5 0.0 copy-done
  115.5 0.6 multiply_add_fusion
  116.1 18.2 %fusion = bf16[1,384,7168]{2,1,0:T(8,128)(2,1)} fusion(f32[256,7168]{1,0:T(8,128)} %param.6, f32[384]{0:T(512)S(1)} %get-tuple-element.4, f32[256]{0:T(256)S(1)} %bitcast.26, f32[384]{0:T(512)S(1)} %get-tuple-element.8, f32[384,256]{0,1:T(8,128)S(1)} %get-tuple-element.9), kind=kOutput, calls=%fused_computation.1 | convolution fusion | flops 8459059200 | bytes 13242368 | tf_op jit(solution)/shard_map/bsn,nd->bsd/dot_general | solution.py:33
  134.3 67.9 %all-reduce.3.cloned.1.call-done = f32[256,7168]{1,0:T(8,128)} async-done(((f32[256,7168]{1,0:T(8,128)}), f32[256,7168]{1,0:T(8,128)}) %all-reduce.3.cloned.1.call-update) | async-done | bytes 7340048 | tf_op jit(solution)/shard_map/psum | solution.py:35
  202.2 6.9 %copy.11 = f32[256,7168]{1,0:T(8,128)} copy(f32[256,7168]{1,0:T(8,128)} %all-reduce.3.cloned.1.call-done) | data formatting | bytes 14680064
  (2 shorter events, 0.0 us)
Async XLA Ops:
  7.2 24.6 %slice-start = ((s8[5505024]{0:T(1024)(128)(4,1)}), s8[1310720]{0:T(1024)(128)(4,1)S(1)}, s32[]{:S(2)}) async-start(s8[5505024]{0:T(1024)(128)(4,1)} %bitcast.22), calls=%async_computation.1 | async-start | bytes 2621440
  7.2 195.1 %all-reduce.3.cloned.1.call-start = ((), (), s32[]{:S(2)}) async-start(), calls=%async_computation | async-start | bytes 14680064 | tf_op jit(solution)/shard_map/psum | solution.py:35
  18.0 13.7 %slice-start.1 = ((s8[5505024]{0:T(1024)(128)(4,1)}), s8[4194304]{0:T(1024)(128)(4,1)S(1)}, s32[]{:S(2)}) async-start(s8[5505024]{0:T(1024)(128)(4,1)} %bitcast.22), calls=%async_computation.2 | async-start | bytes 8388608
  31.8 83.8 %copy-start = (f32[256]{0:T(256)S(1)}, f32[256]{0:T(256)}, u32[]{:S(2)}) copy-start(f32[256]{0:T(256)} %param.7) | copy-start | bytes 3076
Sparse Core Ops, SparseCore 0:
  40.0 162.1 all-reduce.2
where the time goes:
time: 216 us
  blocking collectives  84.3 us (39%)
  waiting for transfers between devices  67.9 us (31%)
  matrix products  39.8 us (18%)
  between operations  14.1 us (7%)
  local copies, waits for them, and re-layouts  7.86 us (4%)
    psum x1, blocking collectives, local_step(): bal_loss = lax.psum(jnp.sum(weight * prob_sums), 'dp')  69 us
    psum x1, waiting for transfers between devices, local_step(): grad_router = lax.psum(grad_part, ('cp', 'dp'))  67.9 us
    dot_general x1, matrix products, local_step(): jnp.einsum('bsn,nd->bsd', grad_logits, router_w, precision=PRECISE, prefe...  18.2 us
    dot_general x1, matrix products, local_step(): jnp.einsum('bsd,nd->bsn', tokens, router_w, precision=PRECISE, preferred_...  13.5 us
    psum x1, blocking collectives, local_step(): seq_counts = lax.psum(piece_counts, 'cp')  9.3 us
    dot_general x1, matrix products, local_step(): jnp.einsum('bsn,bsd->nd', grad_logits, tokens, precision=PRECISE, preferr...  8.08 us
    unnamed x7, local copies, waits for them, and re-layouts  6.94 us
    psum x1, blocking collectives, local_step(): prob_sums = lax.psum(jnp.sum(normed, axis=1), 'cp')  6.01 us
  transfers between devices with their start and end apart: 1, of which 1 were waited for; matrix products, arithmetic and copies ran while one was open for 9% of the time, Pallas kernels for 0%

commit v1 on v0

v1 whole, which is shorter than its diff:
```python
import functools

import jax
import jax.numpy as jnp
from jax import lax
from jax.experimental import pallas as pl
from jax.experimental.pallas import tpu as pltpu
from jax.sharding import PartitionSpec as P

ALPHA = 0.1
GAMMA = 0.001
MESH = pl.DeviceIdType.MESH
LANES = 128
RING = 4
STEPS = (1, RING - 1)
UNIT = 256
DX_COLS = 512
LOAD_COLS = 1024
CHUNKS = 2


def split3(v):
    a = v.astype(jnp.bfloat16)
    r = v - a.astype(jnp.float32)
    b = r.astype(jnp.bfloat16)
    c = (r - b.astype(jnp.float32)).astype(jnp.bfloat16)
    return a, b, c


def dot_nt(a, b):
    return lax.dot_general(a, b, (((1,), (1,)), ((), ())), preferred_element_type=jnp.float32)


def dot_nn(a, b):
    return lax.dot_general(a, b, (((1,), (0,)), ((), ())), preferred_element_type=jnp.float32)


def make_regions(dim):
    tiles = dim // LANES
    num = CHUNKS * 3
    base, extra = divmod(tiles, num)
    widths = [base] * num
    for i in range(extra):
        widths[i * 4 % num if num > 4 else i] += 1
    out, at = [], 0
    for q, wd in enumerate(widths):
        half = (wd + 1) // 2
        out.append((q // 3, q % 3, at * LANES, wd * LANES, half * LANES))
        at += wd
    return out


def kernel(sizes, x_hbm, c_hbm, w_hbm, bias_ref, dw, dx, stat_ref, xv, cv, ws, part, acc, r1, r2, r3, zs, gs, gts, sbuf, srecv,
           load_sem, send_sem, recv_sem):
    experts, dim, toks, choice_num, rows_all, seq_all = sizes
    half_e = experts // 2
    p1 = half_e // RING
    p2 = p1 // RING
    cp = lax.axis_index("cp")
    dp = lax.axis_index("dp")
    core = lax.rem(dp, 2)
    y = lax.rem(dp // 2, RING)
    zc = dp // (2 * RING)
    coord = (cp, y, zc)
    other = 1 - core

    def peer(axis, step):
        if axis == 3:
            return (cp, dp + 1 - 2 * core)
        moved = lax.rem(coord[axis] + step, RING)
        if axis == 0:
            return (moved, dp)
        if axis == 1:
            return (cp, zc * (2 * RING) + moved * 2 + core)
        return (cp, moved * (2 * RING) + y * 2 + core)

    copies = {}
    count = [0]

    def send(key, src, dst, to):
        i = count[0]
        count[0] += 1
        cpy = pltpu.make_async_remote_copy(src_ref=src, dst_ref=dst, send_sem=send_sem.at[i], recv_sem=recv_sem.at[i],
                                           device_id=to, device_id_type=MESH)
        cpy.start()
        copies[key] = cpy

    def arrive(key):
        copies[key].wait_recv()

    nload = dim // LOAD_COLS

    def load(j):
        cols = pl.ds(pl.multiple_of(j * LOAD_COLS, LOAD_COLS), LOAD_COLS)
        return (pltpu.make_async_copy(x_hbm.at[:, cols], xv.at[:, cols], load_sem.at[j]),
                pltpu.make_async_copy(w_hbm.at[:, cols], part.at[:, cols], load_sem.at[nload + j]))

    c_copy = pltpu.make_async_copy(c_hbm, cv, load_sem.at[2 * nload])
    c_copy.start()

    @pl.loop(0, nload)
    def _(j):
        a, b = load(j)
        b.start()
        a.start()

    barrier = pltpu.get_barrier_semaphore()
    for axis in range(3):
        for step in (1, 2, 3):
            pl.semaphore_signal(barrier, inc=1, device_id=peer(axis, step), device_id_type=MESH)
    pl.semaphore_signal(barrier, inc=1, device_id=peer(3, 0), device_id_type=MESH)

    c_copy.wait()
    ids = lax.broadcasted_iota(jnp.int32, (experts, toks), 0)
    hot = jnp.zeros((experts, toks), jnp.float32)
    for i in range(choice_num):
        hot += jnp.where(cv[i:i + 1, :] == ids, 1.0, 0.0)
    counts = dot_nt(jnp.ones((8, toks), jnp.bfloat16), hot.astype(jnp.bfloat16))
    sbuf[0] = counts

    zs[...] = jnp.zeros_like(zs)

    def logits(j):
        a, b = load(j)
        a.wait()
        b.wait()
        cols = pl.ds(pl.multiple_of(j * LOAD_COLS, LOAD_COLS), LOAD_COLS)
        xj = xv[:, cols]
        terms = split3(part[:, cols])
        for i in range(3):
            ws[i, :, cols] = terms[i]
        zs[...] += dot_nt(xj, terms[0]) + dot_nt(xj, terms[1]) + dot_nt(xj, terms[2])

    early = min(2, nload)

    @pl.loop(0, early)
    def _(j):
        logits(j)

    pl.semaphore_wait(barrier, 10)
    for n, step in enumerate((1, 3, 2)):
        send(("s", 0, n), sbuf.at[0], srecv.at[0, n], peer(0, step))

    @pl.loop(early, nload)
    def _(j):
        logits(j)

    for n in range(3):
        arrive(("s", 0, n))
    seq_counts = (sbuf[0] + srecv[0, 2]) + (srecv[0, 0] + srecv[0, 1])
    loss_scale = ALPHA * experts / (rows_all * choice_num * seq_all * seq_all)
    weight = seq_counts[0:1, :] * loss_scale
    sig = lax.logistic(zs[...])
    total = jnp.sum(sig, axis=1, keepdims=True)
    normed = sig / total
    mixed = jnp.sum(normed * weight, axis=1, keepdims=True)
    g = (weight - mixed) * (sig * (1.0 - sig) / total)
    for i, t in enumerate(split3(g)):
        gs[i] = t
    for i, t in enumerate(split3(g.T)):
        gts[i] = t
    loss = jnp.broadcast_to(jnp.sum(mixed, axis=0, keepdims=True), (8, experts))
    is_count = lax.broadcasted_iota(jnp.int32, (8, experts), 0) < 4

    def stat_start(stage):
        sbuf[stage] = stat_val[0]
        if stage == 4:
            send(("s", 4, 0), sbuf.at[4], srecv.at[4, 0], peer(3, 0))
        else:
            for n, step in enumerate((1, 3, 2)):
                send(("s", stage, n), sbuf.at[stage], srecv.at[stage, n], peer(stage - 1, step))

    def stat_end(stage):
        if stage == 4:
            arrive(("s", 4, 0))
            new = sbuf[4] + srecv[4, 0]
        else:
            for n in range(3):
                arrive(("s", stage, n))
            new = (sbuf[stage] + srecv[stage, 2]) + (srecv[stage, 0] + srecv[stage, 1])
            if stage == 1:
                new = jnp.where(is_count, seq_counts, new)
        stat_val[0] = new

    stat_val = [loss]

    regions = make_regions(dim)
    own_e = pl.ds(pl.multiple_of(core * half_e, half_e), half_e)
    oth_e = pl.ds(pl.multiple_of(other * half_e, half_e), half_e)

    def dw_unit(u):
        cols = pl.ds(pl.multiple_of(u * UNIT, UNIT), UNIT)
        xu = xv[:, cols]
        part[:, cols] = dot_nn(gts[0], xu) + dot_nn(gts[1], xu) + dot_nn(gts[2], xu)

    def dx_unit(u):
        cols = pl.ds(pl.multiple_of(u * DX_COLS, DX_COLS), DX_COLS)
        w0, w1, w2 = ws[0, :, cols], ws[1, :, cols], ws[2, :, cols]
        g0, g1, g2 = gs[0], gs[1], gs[2]
        val = dot_nn(g2, w0) + dot_nn(g0, w2) + dot_nn(g1, w1) + dot_nn(g1, w0) + dot_nn(g0, w1) + dot_nn(g0, w0)
        dx[:, cols] = val.astype(jnp.bfloat16)

    dx_done = [0]

    def dx_some(num):
        end = min(dx_done[0] + num, dim // DX_COLS)
        if end > dx_done[0]:
            pl.loop(dx_done[0], end)(dx_unit)
        dx_done[0] = end

    def cols_of(q, h=None):
        _, _, at, wd, hf = regions[q]
        if h is None:
            return pl.ds(at, wd)
        return pl.ds(at, hf) if h == 0 else pl.ds(at + hf, wd - hf)

    def rows(start, size):
        return pl.ds(pl.multiple_of(start, 8), size)

    def axes(q):
        o = regions[q][1]
        return o, (o + 1) % 3, (o + 2) % 3

    def place(q):
        a_ax, b_ax, _ = axes(q)
        return coord[a_ax], coord[b_ax]

    def pair_start(q):
        send(("p", q), part.at[oth_e, cols_of(q)], acc.at[:, cols_of(q)], peer(3, 0))

    def pair_end(q):
        arrive(("p", q))
        acc[:, cols_of(q)] += part[own_e, cols_of(q)]

    def rs1_start(q):
        a_ax = axes(q)[0]
        a, _ = place(q)
        hp = p1 // 2
        for h, step in enumerate(STEPS):
            send(("1o", q, h), acc.at[rows(p1 * lax.rem(a + 2, RING) + hp * h, hp), cols_of(q)],
                 r1.at[0, rows(hp * h, hp), cols_of(q)], peer(a_ax, step))
        for h, step in enumerate(STEPS):
            send(("1d", q, h), acc.at[rows(p1 * lax.rem(a + step, RING) + hp * (1 - h), hp), cols_of(q)],
                 r1.at[1, rows(hp * (1 - h), hp), cols_of(q)], peer(a_ax, step))

    def rs1_mid(q):
        a_ax = axes(q)[0]
        a, _ = place(q)
        hp = p1 // 2
        for h, step in enumerate(STEPS):
            arrive(("1o", q, h))
            here = rows(p1 * lax.rem(a + step, RING) + hp * h, hp)
            acc[here, cols_of(q)] += r1[0, hp * h:hp * h + hp, cols_of(q)]
            send(("1r", q, h), acc.at[here, cols_of(q)], r1.at[2, rows(hp * h, hp), cols_of(q)], peer(a_ax, step))

    def rs1_end(q):
        a, _ = place(q)
        for h in range(2):
            arrive(("1d", q, h))
            arrive(("1r", q, h))
        acc[rows(p1 * a, p1), cols_of(q)] += r1[1, :, cols_of(q)] + r1[2, :, cols_of(q)]

    def rs2_start(q):
        b_ax = axes(q)[1]
        a, b = place(q)
        for h, step in enumerate(STEPS):
            send(("2o", q, h), acc.at[rows(p1 * a + p2 * lax.rem(b + 2, RING), p2), cols_of(q, h)],
                 r2.at[0, :, cols_of(q, h)], peer(b_ax, step))
        for h, step in enumerate(STEPS):
            send(("2d", q, h), acc.at[rows(p1 * a + p2 * lax.rem(b + step, RING), p2), cols_of(q, 1 - h)],
                 r2.at[1, :, cols_of(q, 1 - h)], peer(b_ax, step))

    def rs2_mid(q):
        b_ax = axes(q)[1]
        a, b = place(q)
        for h, step in enumerate(STEPS):
            arrive(("2o", q, h))
            here = rows(p1 * a + p2 * lax.rem(b + step, RING), p2)
            acc[here, cols_of(q, h)] += r2[0, :, cols_of(q, h)]
            send(("2r", q, h), acc.at[here, cols_of(q, h)], r2.at[2, :, cols_of(q, h)], peer(b_ax, step))

    def rs2_end(q):
        a, b = place(q)
        for h in range(2):
            arrive(("2d", q, h))
            arrive(("2r", q, h))
        here = rows(p1 * a + p2 * b, p2)
        acc[here, cols_of(q)] += r2[1, :, cols_of(q)] + r2[2, :, cols_of(q)]
        for n, step in enumerate((1, 3, 2)):
            send(("3", q, n), acc.at[here, cols_of(q)], r3.at[n, :, cols_of(q)], peer(axes(q)[2], step))

    def mine(q):
        a, b = place(q)
        return core * half_e + p1 * a + p2 * b

    def x3_end(q):
        a, b = place(q)
        for n in range(3):
            arrive(("3", q, n))
        val = (acc[rows(p1 * a + p2 * b, p2), cols_of(q)] + r3[2, :, cols_of(q)]) + (r3[0, :, cols_of(q)] + r3[1, :, cols_of(q)])
        dw[rows(mine(q), p2), cols_of(q)] = val
        for kind in range(2):
            for h, step in enumerate(STEPS):
                ref = dw.at[rows(mine(q), p2), cols_of(q, h if kind == 0 else 1 - h)]
                send(("g2", q, kind, h), ref, ref, peer(axes(q)[1], step))

    def ag2_mid(q):
        a, b = place(q)
        for h, step in enumerate(STEPS):
            arrive(("g2", q, 0, h))
            ref = dw.at[rows(core * half_e + p1 * a + p2 * lax.rem(b + (RING - step), RING), p2), cols_of(q, h)]
            send(("g2", q, 2, h), ref, ref, peer(axes(q)[1], step))

    def ag2_end(q):
        for h in range(2):
            arrive(("g2", q, 1, h))
            arrive(("g2", q, 2, h))
        a, _ = place(q)
        hp = p1 // 2
        for kind in range(2):
            for h, step in enumerate(STEPS):
                k = h if kind == 0 else 1 - h
                ref = dw.at[rows(core * half_e + p1 * a + hp * k, hp), cols_of(q)]
                send(("g1", q, kind, h), ref, ref, peer(axes(q)[0], step))
        ref = dw.at[rows(core * half_e + p1 * a, p1), cols_of(q)]
        send(("gp", q, 0), ref, ref, peer(3, 0))

    def to_partner(q, kind, h, shift, k):
        a, _ = place(q)
        hp = p1 // 2
        ref = dw.at[rows(core * half_e + p1 * lax.rem(a + shift, RING) + hp * k, hp), cols_of(q)]
        send(("gp", q, 1, kind, h), ref, ref, peer(3, 0))
        return ref

    def ag1_mid(q):
        for h, step in enumerate(STEPS):
            arrive(("g1", q, 0, h))
            a, _ = place(q)
            hp = p1 // 2
            ref = dw.at[rows(core * half_e + p1 * lax.rem(a + (RING - step), RING) + hp * h, hp), cols_of(q)]
            send(("g1", q, 2, h), ref, ref, peer(axes(q)[0], step))
            to_partner(q, 0, h, RING - step, h)

    def ag1_end(q):
        for h, step in enumerate(STEPS):
            arrive(("g1", q, 1, h))
            to_partner(q, 1, h, RING - step, 1 - h)
        for h, step in enumerate(STEPS):
            arrive(("g1", q, 2, h))
            to_partner(q, 2, h, 2, h)

    def each(chunk, f):
        for q, reg in enumerate(regions):
            if reg[0] == chunk:
                f(q)

    stat_start(1)
    unit = 0
    for q, (_, _, at, wd, _) in enumerate(regions):
        need = -(-(at + wd) // UNIT)
        pl.loop(unit, need)(dw_unit)
        unit = need
        pair_start(q)
        if q >= 1:
            pair_end(q - 1)
            rs1_start(q - 1)
    last = len(regions) - 1
    dx_some(1)
    pair_end(last)
    rs1_start(last)
    stat_end(1)
    stat_start(2)
    dx_some(1)
    each(0, rs1_mid)
    dx_some(2)
    each(1, rs1_mid)
    stat_end(2)
    stat_start(3)
    dx_some(2)
    each(0, rs1_end)
    each(0, rs2_start)
    dx_some(2)
    each(0, rs2_mid)
    each(1, rs1_end)
    each(1, rs2_start)
    stat_end(3)
    stat_start(4)
    dx_some(1)
    each(0, rs2_end)
    each(1, rs2_mid)
    dx_some(1)
    each(0, x3_end)
    each(1, rs2_end)
    dx_some(1)
    each(0, ag2_mid)
    each(0, ag2_end)
    each(1, x3_end)
    dx_some(1)
    each(1, ag2_mid)
    each(0, ag1_mid)
    each(1, ag2_end)
    stat_end(4)
    dx_some(dim)
    loads = stat_val[0][0:1, :]
    gap = rows_all * seq_all * choice_num - loads * experts
    new_bias = bias_ref[...] + GAMMA * jnp.where(gap > 0, 1.0, jnp.where(gap < 0, -1.0, 0.0))
    stat_ref[...] = jnp.where(is_count, jnp.broadcast_to(new_bias, (8, experts)), stat_val[0])
    each(0, ag1_end)
    each(1, ag1_mid)
    each(1, ag1_end)
    for key, cpy in copies.items():
        if key[0] == "gp":
            cpy.wait_recv()
    for cpy in copies.values():
        cpy.wait_send()


def num_copies():
    return 3 * 4 + 1 + CHUNKS * 3 * (1 + 6 + 6 + 3 + 6 + 6 + 7)


def solution(mesh):
    cp_size = mesh.shape["cp"]
    dp_size = mesh.shape["dp"]

    def local_step(tokens, choices, router_w, expert_bias):
        rows_all = tokens.shape[0] * dp_size
        seq_all = tokens.shape[1] * cp_size
        toks, dim = tokens.shape[1:]
        experts = router_w.shape[0]
        choice_num = choices.shape[2]
        sizes = (experts, dim, toks, choice_num, rows_all, seq_all)
        half_e = experts // 2
        nload = dim // LOAD_COLS
        n = num_copies()
        f32, bf16 = jnp.float32, jnp.bfloat16
        anyspace = pl.BlockSpec(memory_space=pl.ANY)
        vm = pl.BlockSpec(memory_space=pltpu.VMEM)
        call = pl.pallas_call(
            functools.partial(kernel, sizes),
            in_specs=[anyspace, anyspace, anyspace, vm],
            out_specs=[vm, vm, vm],
            out_shape=[pltpu.VMEM((experts, dim), f32), pltpu.VMEM((toks, dim), bf16), pltpu.VMEM((8, experts), f32)],
            scratch_shapes=[
                pltpu.VMEM((toks, dim), bf16),
                pltpu.VMEM((choice_num, toks), jnp.int32),
                pltpu.VMEM((3, experts, dim), bf16),
                pltpu.VMEM((experts, dim), f32),
                pltpu.VMEM((half_e, dim), f32),
                pltpu.VMEM((3, half_e // RING, dim), f32),
                pltpu.VMEM((3, half_e // RING // RING, dim), f32),
                pltpu.VMEM((3, half_e // RING // RING, dim), f32),
                pltpu.VMEM((toks, experts), f32),
                pltpu.VMEM((3, toks, experts), bf16),
                pltpu.VMEM((3, experts, toks), bf16),
                pltpu.VMEM((5, 8, experts), f32),
                pltpu.VMEM((5, 3, 8, experts), f32),
                pltpu.SemaphoreType.DMA((2 * nload + 1,)),
                pltpu.SemaphoreType.DMA((n,)),
                pltpu.SemaphoreType.DMA((n,)),
            ],
            compiler_params=pltpu.CompilerParams(collective_id=0, has_side_effects=True, vmem_limit_bytes=44 * 1024 * 1024),
            name="router_step",
        )
        dw, dx, stat = call(tokens[0], choices[0].T, router_w, expert_bias[None, :])
        return stat[4, 0], dw, dx[None], stat[0]

    tok_spec = P("dp", "cp", None)
    return jax.shard_map(local_step, mesh=mesh, in_specs=(tok_spec, tok_spec, P(), P()), out_specs=(P(), P(), tok_spec, P()), check_vma=False)
```

time: 216 us -> 83.7 us (0.39)
  blocking collectives: 84.3 us -> 0 us
  Pallas kernels: 0 us -> 76.3 us
  waiting for transfers between devices: 67.9 us -> 0 us
  matrix products: 39.8 us -> 0 us
  between operations: 14.1 us -> 0.64 us
    psum x3 -> x0, blocking collectives: 84.3 us -> none  [the longest x1 69 us: local_step(): bal_loss = lax.psum(jnp.sum(weight * prob_sums), 'dp')]
    pallas_call x0 -> x1, Pallas kernels: none -> 76.3 us  [local_step(): dw, dx, stat = call(tokens[0], choices[0].T, router_w, expert_bias[None, :])]
    psum x1 -> x0, waiting for transfers between devices: 67.9 us -> none  [local_step(): grad_router = lax.psum(grad_part, ('cp', 'dp'))]
    dot_general x3 -> x0, matrix products: 39.8 us -> none  [the longest x1 18.2 us: local_step(): jnp.einsum('bsn,nd->bsd', grad_logits, router_w, precision=PRECISE, prefe...]
    unnamed x7 -> x2, local copies, waits for them, and re-layouts: 6.94 us -> 5.49 us
  transfers between devices with their start and end apart: 1 -> 0, of which waited for: 1 -> 0; matrix products, arithmetic and copies ran while one was open for 9% -> 0% of each run, Pallas kernels for 0% -> 0%
where the time goes in v1:
time: 83.7 us; the launch traced here: 83.6 us
  Pallas kernels  76.3 us (91%)
  local copies, waits for them, and re-layouts  6.57 us (8%)
    pallas_call x1, Pallas kernels, local_step(): dw, dx, stat = call(tokens[0], choices[0].T, router_w, expert_bias[None, :])  76.3 us
    unnamed x2, local copies, waits for them, and re-layouts  5.49 us

profile of v1, /device:TPU:1, one launch (start us, length us, event | category | flops | bytes accessed | tf_op | source)
XLA Modules:
  0.0 83.6 jit_solution(6274630047536568776)
XLA Ops:
  0.6 76.3 %router_step.1 = (f32[256,7168]{1,0:T(8,128)S(1)}, bf16[384,7168]{1,0:T(8,128)(2,1)S(1)}, f32[8,256]{1,0:T(8,128)S(1)}) custom-call(bf16[384,7168]{1,0:T(8,128)(2,1)} %bitcast.9, s32[8,384]{1,0:T(8,128)} %bitcast.10, f32[256,7168]{1,0:T(8,128)} %w_hbm.1, f32[1,256]{1,0:T(1,128)} %bitcast.12), custom_call_target="tpu_custom_call" | custom-call | tf_op jit(solution)/shard_map/router_step/pallas_call | solution.py:465
  77.0 0.6 slice.7
  77.6 0.5 slice.6
  78.1 3.0 %copy.10 = f32[256,7168]{1,0:T(8,128)} copy(f32[256,7168]{1,0:T(8,128)S(1)} %get-tuple-element.11) | data formatting | bytes 14680064
  81.1 2.4 %copy.11 = bf16[1,384,7168]{2,1,0:T(8,128)(2,1)} copy(bf16[1,384,7168]{2,1,0:T(8,128)(2,1)S(1)} %bitcast.8) | data formatting | bytes 11010048
